TPU v7x, 32 devices: a whole 2x2x4 slice. The times are simulated.
32 devices in a mesh: groups: 2 (over y), dp: 2 (over core), tensor: 8 (over z, x).
Axes of the slice: x: 2, y: 2, z: 4, core: 2. Of those that a mesh axis runs over, the one named last changes fastest.
Arguments:
- hidden_in: bfloat16 [4, 1024, 5120], P(('groups', 'dp'), 'tensor'), parts along dimension 0, may hold values from -40 to 40
- first_values: bfloat16 [4, 1024, 1024], P(('groups', 'dp'), 'tensor'), parts along dimension 0, may hold values from -6 to 6
- qkv_weight: bfloat16 [5120, 3, 1024], P(None, None, 'tensor'), may hold values from -1 to 1
- out_weight: bfloat16 [1024, 5120], P('tensor'), may hold values from -0.1875 to 0.1875
- mix_table: float32 [8, 2], replicated, may hold values from 0.2 to 1
- mix_index: int32 [8], P('tensor'), may hold values from 0 to 7
- lengths: int32 [4], P(('groups', 'dp')), parts along dimension 0, may hold values from 256 to 1024
Outputs:
- attn_out: bfloat16 [4, 1024, 5120], P(('groups', 'dp'), 'tensor'), parts along dimension 0
There are 2 independent parts, one for each index of `groups`. A program takes and returns all parts, laid end to end along the dimension named above; an argument that names none is the same for every part. Nothing has to cross between parts.
All inputs are finite; a program needn't handle non-finite values.
Results may differ from a plain program's by a relative error of at most 0.0077.
Values may be sent and summed in bfloat16 or wider, within the bound.
A program may use at most 128 MiB of HBM per device.

v0:
```python
import functools
import math

import jax
import jax.numpy as jnp
from jax import lax
from jax.experimental import pallas as pl
from jax.experimental.pallas import tpu as pltpu
from jax.sharding import PartitionSpec as P

NEG_FILL = -1e30
PAIR = 2


def attention(queries, key_rows, mixed_values, valid_length, head_size):
    total_rows = queries.shape[0]
    positions = jnp.arange(total_rows, dtype=jnp.int32)
    score_scale = 1.0 / math.sqrt(head_size)
    block_rows = min(512, total_rows)
    outputs = []
    for first_row in range(0, total_rows, block_rows):
        stop = first_row + block_rows
        scores = (
            jnp.einsum(
                "qhd,khd->hqk",
                queries[first_row:stop],
                key_rows[:stop],
                preferred_element_type=jnp.float32,
            )
            * score_scale
        )
        keys_at, rows_at = positions[:stop], positions[first_row:stop]
        allowed = (keys_at[None, :] <= rows_at[:, None]) & (keys_at[None, :] < valid_length)
        scores = jnp.where(allowed[None], scores, NEG_FILL)
        row_max = jnp.max(scores, axis=2, keepdims=True)
        raised = jnp.exp(scores - row_max)
        weights = (raised / jnp.sum(raised, axis=2, keepdims=True)).astype(jnp.bfloat16)
        outputs.append(
            jnp.einsum(
                "hqk,khd->qhd", weights, mixed_values[:stop], preferred_element_type=jnp.float32
            ).astype(jnp.bfloat16)
        )
    return jnp.concatenate(outputs, axis=0)


def body(hidden_in, first_values, qkv_weight, out_weight, mix_table, mix_index, lengths):
    local_rows = hidden_in[0]
    own_rows, model_width = local_rows.shape
    head_width = qkv_weight.shape[2]
    heads_here = mix_index.shape[0]
    head_size = head_width // heads_here
    ranks = lax.axis_size("tensor")
    cores = lax.axis_size("dp")
    rank = lax.axis_index("tensor")
    core = lax.axis_index("dp")
    side = rank % PAIR
    line = ranks // PAIR
    swap_pair = [(r, r ^ 1) for r in range(ranks)]
    swap_core = [(c, c ^ 1) for c in range(cores)]

    own_w = qkv_weight.reshape(model_width, 3 * head_width)
    half = model_width // 2
    sent = lax.dynamic_slice_in_dim(own_w, core * half, half, 0)
    got = lax.ppermute(sent, "tensor", swap_pair)
    got_other = lax.ppermute(got, "dp", swap_core)
    pair_w = jnp.where(
        core == 0,
        jnp.concatenate([got, got_other], axis=0),
        jnp.concatenate([got_other, got], axis=0),
    )

    lines = [[s + PAIR * i for i in range(line)] for s in range(PAIR)]
    rows = lax.all_gather(local_rows, "tensor", axis=0, tiled=True, axis_index_groups=lines)
    for_pair = jnp.dot(rows, pair_w, preferred_element_type=jnp.float32).astype(jnp.bfloat16)
    from_pair = lax.ppermute(for_pair, "tensor", swap_pair)
    ours = jnp.dot(rows, own_w, preferred_element_type=jnp.float32).astype(jnp.bfloat16)
    ours = ours.reshape(line, own_rows, 3 * head_width)
    from_pair = from_pair.reshape(line, own_rows, 3 * head_width)
    projected = jnp.where(
        side == 0,
        jnp.stack([ours, from_pair], axis=1),
        jnp.stack([from_pair, ours], axis=1),
    )
    total_rows = ranks * own_rows
    split_parts = projected.reshape(total_rows, 3, heads_here, head_size)

    relaid = lax.all_to_all(first_values[0], "tensor", split_axis=1, concat_axis=0, tiled=True)
    firsts = relaid.reshape(total_rows, heads_here, head_size)
    levels = mix_table.shape[0]
    one_hot = (mix_index[:, None] == jnp.arange(levels, dtype=jnp.int32)[None, :]).astype(
        jnp.float32
    )
    weights_mix = jnp.dot(one_hot, mix_table, precision=lax.Precision.HIGHEST)
    mixed_values = (
        weights_mix[None, :, 0:1] * split_parts[:, 2].astype(jnp.float32)
        + weights_mix[None, :, 1:2] * firsts.astype(jnp.float32)
    ).astype(jnp.bfloat16)
    attended = attention(
        split_parts[:, 0], split_parts[:, 1], mixed_values, lengths[0], head_size
    ).reshape(total_rows, head_width)

    gathered_bytes = ranks * out_weight.size * 2
    summed_bytes = total_rows * model_width * 4
    if gathered_bytes > summed_bytes:
        kept_rows = lax.psum_scatter(
            jnp.dot(attended, out_weight, preferred_element_type=jnp.float32),
            "tensor",
            scatter_dimension=0,
            tiled=True,
        )
        return kept_rows.astype(jnp.bfloat16)[None]

    part = head_width // 2
    own_part = lax.dynamic_slice_in_dim(out_weight, core * part, part, 0)
    mine = lax.all_gather(own_part, "tensor", axis=0, tiled=True)
    other = lax.ppermute(mine, "dp", swap_core)
    kept = lax.all_to_all(attended, "tensor", split_axis=0, concat_axis=1, tiled=True)
    kept = kept.reshape(own_rows, ranks, 2, part)
    low = kept[:, :, 0].reshape(own_rows, ranks * part)
    high = kept[:, :, 1].reshape(own_rows, ranks * part)
    out = jnp.dot(
        jnp.where(core == 0, low, high), mine, preferred_element_type=jnp.float32
    ) + jnp.dot(jnp.where(core == 0, high, low), other, preferred_element_type=jnp.float32)
    return out.astype(jnp.bfloat16)[None]


PIECES = 2
MESH = pl.DeviceIdType.MESH


def gather_project(
    line, rows_ref, w_ref, ow_ref, fv_ref, qkv_ref, wf_ref, fo_ref,
    hid, both_w, own_o, staged,
    load_sem, hs_sem, hr_sem, ws_sem, wr_sem, os_sem, or_sem, xs_sem, xr_sem,
    ys_sem, yr_sem, ds_sem, dr_sem, es_sem, er_sem, ps_sem, pr_sem, fs_sem, fr_sem,
):
    group, core, rank = lax.axis_index("groups"), lax.axis_index("dp"), lax.axis_index("tensor")
    spot, side = rank // PAIR, rank % PAIR
    steps = line - 1
    own_rows, width = rows_ref.shape
    half = width // 2
    quarter = ow_ref.shape[0] // 4
    mine = group * 2 + core
    across = (1 - group) * 2 + core
    left, right = (group, core, rank - PAIR), (group, core, rank + PAIR)
    partner = (group, core, spot * PAIR + 1 - side)
    opposite = (1 - group, core, rank)
    sibling = (group, 1 - core, rank)
    has_left, has_right = spot > 0, spot < steps

    barrier = pltpu.get_barrier_semaphore()
    ranks = line * PAIR
    head = w_ref.shape[2]
    peers = [(group, core, (rank + o) % ranks) for o in range(1, ranks)]
    for there in peers + [opposite, sibling]:
        pl.semaphore_signal(barrier, inc=1, device_id=there, device_id_type=MESH)

    loads = [
        pltpu.make_async_copy(rows_ref, hid.at[spot], load_sem.at[0]),
        pltpu.make_async_copy(ow_ref, own_o, load_sem.at[1]),
        pltpu.make_async_copy(w_ref, both_w.at[:, :, pl.ds(0, head)], load_sem.at[2]),
        pltpu.make_async_copy(
            fv_ref.at[:, pl.ds(pl.multiple_of(rank * head, head), head)], fo_ref.at[rank], load_sem.at[4]
        ),
    ]
    for load in loads:
        load.start()
    pl.semaphore_wait(barrier, ranks + 1)

    def send(src, dst, s_sem, r_sem, there):
        return pltpu.make_async_remote_copy(
            src_ref=src, dst_ref=dst, send_sem=s_sem, recv_sem=r_sem, device_id=there, device_id_type=MESH
        )

    def wf(column, q):
        return wf_ref.at[column, pl.ds(q * quarter, quarter), :]

    def chunk(way, k):
        return spot - 1 - k if way == 0 else spot + 1 + k

    def arrives(way, k):
        return k < spot if way == 0 else spot + 1 + k < line

    def leaves(way, k):
        if way == 0:
            return jnp.logical_and(k <= spot, has_right)
        return jnp.logical_and(spot + k < line, has_left)

    def carried(way, k):
        return spot - k if way == 0 else spot + k

    def ahead(way):
        return right if way == 0 else left

    piece = own_rows // PIECES

    def hid_copy(way, k, p, at):
        cut = pl.ds(p * piece, piece)
        source = rows_ref.at[cut, :] if k == 0 else hid.at[at, cut, :]
        return send(source, hid.at[at, cut, :], hs_sem.at[way, k, p], hr_sem.at[way, k, p], ahead(way))

    def out_copy(way, k, at):
        column = at * PAIR + side
        source = ow_ref.at[pl.ds(mine * quarter, quarter), :] if k == 0 else wf(column, mine)
        return send(source, wf(column, mine), os_sem.at[way, k], or_sem.at[way, k], ahead(way))

    def pair_copy(slot, column, source):
        return send(source, wf(column, mine), xs_sem.at[slot], xr_sem.at[slot], partner)

    def y_copy(slot, column):
        return send(wf(column, mine), wf(column, mine), ys_sem.at[slot], yr_sem.at[slot], opposite)

    def y_arrival(slot, column):
        return send(wf(column, across), wf(column, across), ys_sem.at[slot], yr_sem.at[slot], opposite)

    def d_copy(slot, column, q):
        return send(wf(column, q), wf(column, q), ds_sem.at[slot], dr_sem.at[slot], sibling)

    def e_copy(slot, column, q):
        return send(wf(column, q), wf(column, q), es_sem.at[slot], er_sem.at[slot], sibling)

    def spread(slot, column):
        y_copy(slot, column).start()
        d_copy(slot, column, mine).start()

    last = 2 * steps
    all_slots = [(way * steps + k, way, k) for k in range(steps) for way in (0, 1)]
    partner_column = spot * PAIR + 1 - side

    for way in (0, 1):

        @pl.when(leaves(way, 0))
        def _():
            out_copy(way, 0, spot).start()
            for p in range(PIECES):
                hid_copy(way, 0, p, spot).start()

    own_quarter = ow_ref.at[pl.ds(mine * quarter, quarter), :]
    pair_copy(last, rank, own_quarter).start()
    cut_w = pl.ds(core * half, half)
    other_w = pl.ds((1 - core) * half, half)
    lanes = pl.ds(head, head)
    w_out = send(w_ref.at[:, cut_w, :], both_w.at[:, cut_w, lanes], ws_sem.at[0], wr_sem.at[0], partner)
    first_copies = [
        send(
            fv_ref.at[:, pl.ds(pl.multiple_of(there[2] * head, head), head)],
            fo_ref.at[rank], fs_sem.at[o], fr_sem.at[o], there,
        )
        for o, there in enumerate(peers)
    ]
    w_out.start()
    for copy in first_copies:
        copy.start()
    for load in loads:
        load.wait()
    keep = pltpu.make_async_copy(own_o, wf_ref.at[rank], load_sem.at[3])
    keep.start()

    def project(slot, at):
        def one(j, carry):
            total = jnp.dot(hid[at], both_w[j], preferred_element_type=jnp.float32)
            staged[slot, j] = total[:, head:].astype(jnp.bfloat16)
            qkv_ref[j, at, side] = total[:, :head].astype(jnp.bfloat16)
            return carry

        lax.fori_loop(0, 3, one, 0)

    def swap_copy(slot, at):
        return send(
            staged.at[slot], qkv_ref.at[:, at, side], ps_sem.at[slot], pr_sem.at[slot], partner
        )

    def swap_arrival(slot, at):
        return send(
            staged.at[slot], qkv_ref.at[:, at, 1 - side], ps_sem.at[slot], pr_sem.at[slot], partner
        )

    for k in range(steps):
        for way in (0, 1):

            @pl.when(arrives(way, k))
            def _():
                at = chunk(way, k)
                out_copy(way, k, at).wait_recv()
                if k + 1 < steps:

                    @pl.when(leaves(way, k + 1))
                    def _():
                        out_copy(way, k + 1, at).start()

                slot = way * steps + k
                column = at * PAIR + side
                pair_copy(slot, column, wf(column, mine)).start()
                spread(slot, column)

        for p in range(PIECES):
            for way in (0, 1):

                @pl.when(arrives(way, k))
                def _():
                    at = chunk(way, k)
                    hid_copy(way, k, p, at).wait_recv()
                    if k + 1 < steps:

                        @pl.when(leaves(way, k + 1))
                        def _():
                            hid_copy(way, k + 1, p, at).start()

            due = ([k - 1] if k > 0 else []) + ([k] if k == steps - 1 else [])
            for e in due if p == 0 else []:
                for way in (0, 1):

                    @pl.when(arrives(way, e))
                    def _():
                        column = chunk(way, e) * PAIR + 1 - side
                        pair_copy(way * steps + e, column, wf(column, mine)).wait_recv()
                        spread(last + way * steps + e, column)

        if k == 0:
            pair_copy(last, partner_column, wf(partner_column, mine)).wait_recv()
            spread(2 * last, partner_column)
            send(
                w_ref.at[:, cut_w, :], both_w.at[:, cut_w, lanes], ws_sem.at[0], wr_sem.at[0], partner
            ).wait_recv()
            w_side = send(
                both_w.at[:, cut_w, lanes], both_w.at[:, cut_w, lanes], ws_sem.at[1], wr_sem.at[1], sibling
            )
            w_side.start()
            send(
                both_w.at[:, other_w, lanes], both_w.at[:, other_w, lanes], ws_sem.at[1], wr_sem.at[1], sibling
            ).wait_recv()
            project(last, spot)
        for way in (0, 1):

            @pl.when(arrives(way, k))
            def _():
                at = chunk(way, k)
                slot = way * steps + k
                project(slot, at)
                swap_copy(slot, at).start()

        if k == 0:
            swap_copy(last, spot).start()

    columns = [(2 * last, partner_column, None)]
    for slot, way, k in all_slots:
        columns.append((slot, chunk(way, k) * PAIR + side, (way, k)))
        columns.append((last + slot, chunk(way, k) * PAIR + 1 - side, (way, k)))

    def each(action):
        for slot, column, when in columns:
            if when is None:
                action(slot, column)
            else:

                @pl.when(arrives(*when))
                def _():
                    action(slot, column)

    def pass_on(slot, column):
        y_arrival(slot, column).wait_recv()
        e_copy(slot, column, across).start()

    def finish(slot, column):
        sib_mine = group * 2 + 1 - core
        sib_across = (1 - group) * 2 + 1 - core
        d_copy(slot, column, sib_mine).wait_recv()
        e_copy(slot, column, sib_across).wait_recv()
        y_copy(slot, column).wait_send()
        d_copy(slot, column, mine).wait_send()
        e_copy(slot, column, across).wait_send()

    each(pass_on)
    each(finish)
    for slot, way, k in all_slots:

        @pl.when(arrives(way, k))
        def _():
            at = chunk(way, k)
            swap_arrival(slot, at).wait_recv()
            swap_copy(slot, at).wait_send()
            column = at * PAIR + side
            pair_copy(slot, column, wf(column, mine)).wait_send()

        @pl.when(leaves(way, k))
        def _():
            at = carried(way, k)
            out_copy(way, k, at).wait_send()
            for p in range(PIECES):
                hid_copy(way, k, p, at).wait_send()

    swap_arrival(last, spot).wait_recv()
    swap_copy(last, spot).wait_send()
    pair_copy(last, rank, own_quarter).wait_send()
    w_out.wait_send()
    w_side.wait_send()
    keep.wait()
    for o in range(ranks - 1):
        send(
            fv_ref.at[:, pl.ds(0, head)], fo_ref.at[(rank + ranks - 1 - o) % ranks],
            fs_sem.at[o], fr_sem.at[o], peers[o],
        ).wait_recv()
    for copy in first_copies:
        copy.wait_send()


def exchange(ranks, att_ref, kept_ref, load_sem, s_sem, r_sem):
    group, core, rank = lax.axis_index("groups"), lax.axis_index("dp"), lax.axis_index("tensor")
    rows, head = kept_ref.shape[0], att_ref.shape[1]
    peers = [(group, core, (rank + o) % ranks) for o in range(1, ranks)]
    barrier = pltpu.get_barrier_semaphore()
    for there in peers:
        pl.semaphore_signal(barrier, inc=1, device_id=there, device_id_type=MESH)
    pl.semaphore_wait(barrier, ranks - 1)

    def block(r):
        return att_ref.at[pl.ds(pl.multiple_of(r * rows, rows), rows), :]

    def column(r):
        return kept_ref.at[:, pl.ds(pl.multiple_of(r * head, head), head)]

    def copy(o, r):
        return pltpu.make_async_remote_copy(
            src_ref=block(peers[o][2]), dst_ref=column(r), send_sem=s_sem.at[o], recv_sem=r_sem.at[o],
            device_id=peers[o], device_id_type=MESH,
        )

    for o in range(ranks - 1):
        copy(o, rank).start()
    own = pltpu.make_async_copy(block(rank), column(rank), load_sem)
    own.start()
    own.wait()
    for o in range(ranks - 1):
        copy(o, (rank + ranks - 1 - o) % ranks).wait_recv()
    for o in range(ranks - 1):
        copy(o, rank).wait_send()


def to_positions(attended, ranks):
    total_rows, head_width = attended.shape
    dma = pltpu.SemaphoreType.DMA
    return pl.pallas_call(
        functools.partial(exchange, ranks),
        out_shape=jax.ShapeDtypeStruct((total_rows // ranks, ranks * head_width), attended.dtype),
        in_specs=[pl.BlockSpec(memory_space=pltpu.VMEM)],
        out_specs=pl.BlockSpec(memory_space=pltpu.VMEM),
        scratch_shapes=[dma, dma((ranks - 1,)), dma((ranks - 1,))],
        compiler_params=pltpu.CompilerParams(
            collective_id=1, has_side_effects=True, vmem_limit_bytes=8 * 1024 * 1024
        ),
    )(attended)


def gathered(local_rows, w3, out_weight, firsts, ranks):
    line = ranks // PAIR
    steps = line - 1
    own_rows, width = local_rows.shape
    head_width = w3.shape[2]
    kind = local_rows.dtype
    dma = pltpu.SemaphoreType.DMA
    slots, wide = 2 * steps + 1, 4 * steps + 1
    anywhere = pl.BlockSpec(memory_space=pltpu.HBM)
    return pl.pallas_call(
        functools.partial(gather_project, line),
        out_shape=(
            jax.ShapeDtypeStruct((3, line, PAIR, own_rows, head_width), kind),
            jax.ShapeDtypeStruct((ranks,) + out_weight.shape, kind),
            jax.ShapeDtypeStruct((ranks, own_rows, head_width), kind),
        ),
        in_specs=[anywhere] * 4,
        out_specs=(
            pl.BlockSpec(memory_space=pltpu.VMEM),
            anywhere,
            pl.BlockSpec(memory_space=pltpu.VMEM),
        ),
        scratch_shapes=[
            pltpu.VMEM((line, own_rows, width), kind),
            pltpu.VMEM(w3.shape[:2] + (2 * head_width,), kind),
            pltpu.VMEM(out_weight.shape, kind),
            pltpu.VMEM((slots, 3, own_rows, head_width), kind),
            dma((5,)),
            dma((2, steps, PIECES)), dma((2, steps, PIECES)),
            dma((2,)), dma((2,)),
            dma((2, steps)), dma((2, steps)),
            dma((slots,)), dma((slots,)),
            dma((wide,)), dma((wide,)),
            dma((wide,)), dma((wide,)),
            dma((wide,)), dma((wide,)),
            dma((slots,)), dma((slots,)),
            dma((ranks - 1,)), dma((ranks - 1,)),
        ],
        compiler_params=pltpu.CompilerParams(
            collective_id=0, has_side_effects=True, vmem_limit_bytes=48 * 1024 * 1024
        ),
    )(local_rows, w3, out_weight, firsts)


def mix(values, firsts, mix_table, mix_index):
    levels = mix_table.shape[0]
    one_hot = (mix_index[:, None] == jnp.arange(levels, dtype=jnp.int32)[None, :]).astype(
        jnp.float32
    )
    weights_mix = jnp.dot(one_hot, mix_table, precision=lax.Precision.HIGHEST)
    return (
        weights_mix[None, :, 0:1] * values.astype(jnp.float32)
        + weights_mix[None, :, 1:2] * firsts.astype(jnp.float32)
    ).astype(jnp.bfloat16)


def body_gathered(hidden_in, first_values, qkv_weight, out_weight, mix_table, mix_index, lengths):
    local_rows = hidden_in[0]
    own_rows = local_rows.shape[0]
    ranks = lax.axis_size("tensor")
    total_rows = ranks * own_rows
    heads_here = mix_index.shape[0]
    head_width = qkv_weight.shape[2]
    head_size = head_width // heads_here
    qkv, full_out, relaid = gathered(
        local_rows, qkv_weight.transpose(1, 0, 2), out_weight, first_values[0], ranks
    )
    firsts = relaid.reshape(total_rows, heads_here, head_size)
    qkv = qkv.reshape(3, total_rows, heads_here, head_size)
    mixed_values = mix(qkv[2], firsts, mix_table, mix_index)
    attended = attention(qkv[0], qkv[1], mixed_values, lengths[0], head_size)
    attended = attended.reshape(total_rows, head_width)
    kept = to_positions(attended, ranks)
    weights = full_out.reshape(ranks * head_width, full_out.shape[2])
    return jnp.dot(kept, weights, preferred_element_type=jnp.float32).astype(jnp.bfloat16)[None]


def chosen(hidden_in, first_values, qkv_weight, out_weight, mix_table, mix_index, lengths):
    args = (hidden_in, first_values, qkv_weight, out_weight, mix_table, mix_index, lengths)
    ranks = lax.axis_size("tensor")
    total_rows = ranks * hidden_in.shape[1]
    fits = ranks * out_weight.size * 2 <= total_rows * hidden_in.shape[2] * 4
    two = lax.axis_size("groups") == 2 and lax.axis_size("dp") == 2
    if fits and two:
        return body_gathered(*args)
    return body(*args)


def solution(mesh):
    placed = (
        P(("groups", "dp"), "tensor", None),
        P(("groups", "dp"), "tensor", None),
        P(None, None, "tensor"),
        P("tensor", None),
        P(),
        P("tensor"),
        P(("groups", "dp")),
    )
    return jax.shard_map(
        chosen,
        mesh=mesh,
        in_specs=placed,
        out_specs=P(("groups", "dp"), "tensor", None),
        check_vma=False,
    )
```

profile of v0, /device:TPU:0, one launch (start us, length us, event | category | flops | bytes accessed | tf_op | source)
XLA Modules:
  0.0 145.6 jit_solution(6871755082673889886)
XLA Ops:
  0.0 0.0 copy-start
  1.3 0.0 copy-done
  1.3 0.1 fusion.10
  1.4 0.6 fusion.14
  2.1 0.0 copy-start.4
  2.1 0.0 copy-start.1
  2.1 1.3 copy-done.1
  3.4 0.0 copy-start.2
  3.4 1.3 copy-done.2
  4.7 0.0 copy-start.3
  4.7 0.9 copy-done.3
  5.7 124.0 %shard_map.73 = (bf16[3,4,2,128,128]{4,3,2,1,0:T(8,128)(2,1)S(1)}, bf16[8,128,5120]{2,1,0:T(8,128)(2,1)}, bf16[8,128,128]{2,1,0:T(8,128)(2,1)S(1)}) custom-call(bf16[128,5120]{1,0:T(8,128)(2,1)S(1)} %bitcast.46, bf16[3,5120,128]{2,1,0:T(8,128)(2,1)} %bitcast.51, bf16[128,5120]{1,0:T(8,128)(2,1)S(1)} %copy-done.2, bf16[128,1024]{1,0:T(8,128)(2,1)S(1)} %bitcast.47), custom_call_target="tpu_custom_call" | custom-call | tf_op jit(solution)/shard_map/pallas_call | solution.py:463
  129.7 0.0 copy-done.4
  129.7 0.0 slice-start.3
  129.8 0.7 convert_multiply_fusion
  130.5 0.8 convert_multiply_fusion.1
  131.2 0.0 slice-done.3
  131.3 0.4 fusion.16
  131.7 0.2 fusion.6
  131.9 0.0 slice-start
  131.9 0.4 fusion.4
  132.3 0.0 slice-start.1
  132.3 0.8 fusion.15
  133.0 0.5 fusion.2
  133.6 0.0 slice-start.2
  133.6 0.5 fusion.5
  134.1 8.8 %shard_map.74 = bf16[128,1024]{1,0:T(8,128)(2,1)S(1)} custom-call(bf16[1024,128]{1,0:T(8,128)(2,1)S(1)} %maximum_bitcast_fusion.att_ref), custom_call_target="tpu_custom_call" | custom-call | tf_op jit(solution)/shard_map/pallas_call | solution.py:442
  143.0 0.0 slice-done
  143.0 0.0 slice-done.1
  143.0 0.0 slice-done.2
  143.0 2.6 %fusion = bf16[1,128,5120]{2,1,0:T(8,128)(2,1)} fusion(bf16[128,1024]{1,0:T(8,128)(2,1)S(1)} %shard_map.74, bf16[1024,5120]{1,0:T(8,128)(2,1)S(1)} %bitcast.50), kind=kOutput, calls=%fused_computation.1 | convolution fusion | flops 1342832640 | bytes 12058624 | tf_op jit(solution)/shard_map/dot_general | solution.py:528
  (9 shorter events, 0.1 us)
Async XLA Ops:
  0.0 1.3 copy-start
  2.1 127.7 %copy-start.4 = (s32[1024]{0:T(1024)}, s32[1024]{0:T(1024)S(1)}, u32[]{:S(2)}) copy-start(s32[1024]{0:T(1024)S(1)} %iota.19) | copy-start | bytes 12292
  2.1 1.3 copy-start.1
  3.4 1.3 copy-start.2
  4.7 0.9 copy-start.3
  129.7 1.5 %slice-start.3 = ((s32[1024]{0:T(1024)}), s32[512]{0:T(512)S(1)}, s32[]{:S(2)}) async-start(s32[1024]{0:T(1024)} %copy-done.4), calls=%async_computation.3 | async-start | bytes 4096 | tf_op jit(solution)/shard_map/slice | solution.py:32
  131.9 11.1 %slice-start = ((s8[10485760]{0:T(1024)(128)(4,1)}), s8[4194304]{0:T(1024)(128)(4,1)S(1)}, s32[]{:S(2)}) async-start(s8[10485760]{0:T(1024)(128)(4,1)} %bitcast.48), calls=%async_computation | async-start | bytes 8388608
  132.3 10.7 %slice-start.1 = ((s8[10485760]{0:T(1024)(128)(4,1)}), s8[4194304]{0:T(1024)(128)(4,1)S(1)}, s32[]{:S(2)}) async-start(s8[10485760]{0:T(1024)(128)(4,1)} %bitcast.48), calls=%async_computation.1 | async-start | bytes 8388608
  133.6 9.5 %slice-start.2 = ((s8[10485760]{0:T(1024)(128)(4,1)}), s8[2097152]{0:T(1024)(128)(4,1)S(1)}, s32[]{:S(2)}) async-start(s8[10485760]{0:T(1024)(128)(4,1)} %bitcast.48), calls=%async_computation.2 | async-start | bytes 4194304
where the time goes:
time: 146 us
  Pallas kernels  133 us (91%)
  matrix products  4.82 us (3%)
  local copies, waits for them, and re-layouts  4.27 us (3%)
  other arithmetic  2.17 us (1%)
  between operations  1.5 us (1%)
    pallas_call x1, Pallas kernels, gathered(): pl.pallas_call(functools.partial(gather_project, line), out_shape=(jax.Sh...  124 us
    pallas_call x1, Pallas kernels, to_positions(): pl.pallas_call(functools.partial(exchange, ranks), out_shape=jax.ShapeDty...  8.84 us
    unnamed x16, local copies, waits for them, and re-layouts  3.6 us

commit v1 on v0

v1 whole, which is shorter than its diff:
```python
import functools
import math

import jax
import jax.numpy as jnp
from jax import lax
from jax.experimental import pallas as pl
from jax.experimental.pallas import tpu as pltpu
from jax.sharding import PartitionSpec as P

NEG_FILL = -1e30
PAIR = 2


def attention(queries, key_rows, mixed_values, valid_length, head_size):
    total_rows = queries.shape[0]
    positions = jnp.arange(total_rows, dtype=jnp.int32)
    score_scale = 1.0 / math.sqrt(head_size)
    block_rows = min(512, total_rows)
    outputs = []
    for first_row in range(0, total_rows, block_rows):
        stop = first_row + block_rows
        scores = (
            jnp.einsum(
                "qhd,khd->hqk",
                queries[first_row:stop],
                key_rows[:stop],
                preferred_element_type=jnp.float32,
            )
            * score_scale
        )
        keys_at, rows_at = positions[:stop], positions[first_row:stop]
        allowed = (keys_at[None, :] <= rows_at[:, None]) & (keys_at[None, :] < valid_length)
        scores = jnp.where(allowed[None], scores, NEG_FILL)
        row_max = jnp.max(scores, axis=2, keepdims=True)
        raised = jnp.exp(scores - row_max)
        weights = (raised / jnp.sum(raised, axis=2, keepdims=True)).astype(jnp.bfloat16)
        outputs.append(
            jnp.einsum(
                "hqk,khd->qhd", weights, mixed_values[:stop], preferred_element_type=jnp.float32
            ).astype(jnp.bfloat16)
        )
    return jnp.concatenate(outputs, axis=0)


def body(hidden_in, first_values, qkv_weight, out_weight, mix_table, mix_index, lengths):
    local_rows = hidden_in[0]
    own_rows, model_width = local_rows.shape
    head_width = qkv_weight.shape[2]
    heads_here = mix_index.shape[0]
    head_size = head_width // heads_here
    ranks = lax.axis_size("tensor")
    cores = lax.axis_size("dp")
    rank = lax.axis_index("tensor")
    core = lax.axis_index("dp")
    side = rank % PAIR
    line = ranks // PAIR
    swap_pair = [(r, r ^ 1) for r in range(ranks)]
    swap_core = [(c, c ^ 1) for c in range(cores)]

    own_w = qkv_weight.reshape(model_width, 3 * head_width)
    half = model_width // 2
    sent = lax.dynamic_slice_in_dim(own_w, core * half, half, 0)
    got = lax.ppermute(sent, "tensor", swap_pair)
    got_other = lax.ppermute(got, "dp", swap_core)
    pair_w = jnp.where(
        core == 0,
        jnp.concatenate([got, got_other], axis=0),
        jnp.concatenate([got_other, got], axis=0),
    )

    lines = [[s + PAIR * i for i in range(line)] for s in range(PAIR)]
    rows = lax.all_gather(local_rows, "tensor", axis=0, tiled=True, axis_index_groups=lines)
    for_pair = jnp.dot(rows, pair_w, preferred_element_type=jnp.float32).astype(jnp.bfloat16)
    from_pair = lax.ppermute(for_pair, "tensor", swap_pair)
    ours = jnp.dot(rows, own_w, preferred_element_type=jnp.float32).astype(jnp.bfloat16)
    ours = ours.reshape(line, own_rows, 3 * head_width)
    from_pair = from_pair.reshape(line, own_rows, 3 * head_width)
    projected = jnp.where(
        side == 0,
        jnp.stack([ours, from_pair], axis=1),
        jnp.stack([from_pair, ours], axis=1),
    )
    total_rows = ranks * own_rows
    split_parts = projected.reshape(total_rows, 3, heads_here, head_size)

    relaid = lax.all_to_all(first_values[0], "tensor", split_axis=1, concat_axis=0, tiled=True)
    firsts = relaid.reshape(total_rows, heads_here, head_size)
    levels = mix_table.shape[0]
    one_hot = (mix_index[:, None] == jnp.arange(levels, dtype=jnp.int32)[None, :]).astype(
        jnp.float32
    )
    weights_mix = jnp.dot(one_hot, mix_table, precision=lax.Precision.HIGHEST)
    mixed_values = (
        weights_mix[None, :, 0:1] * split_parts[:, 2].astype(jnp.float32)
        + weights_mix[None, :, 1:2] * firsts.astype(jnp.float32)
    ).astype(jnp.bfloat16)
    attended = attention(
        split_parts[:, 0], split_parts[:, 1], mixed_values, lengths[0], head_size
    ).reshape(total_rows, head_width)

    gathered_bytes = ranks * out_weight.size * 2
    summed_bytes = total_rows * model_width * 4
    if gathered_bytes > summed_bytes:
        kept_rows = lax.psum_scatter(
            jnp.dot(attended, out_weight, preferred_element_type=jnp.float32),
            "tensor",
            scatter_dimension=0,
            tiled=True,
        )
        return kept_rows.astype(jnp.bfloat16)[None]

    part = head_width // 2
    own_part = lax.dynamic_slice_in_dim(out_weight, core * part, part, 0)
    mine = lax.all_gather(own_part, "tensor", axis=0, tiled=True)
    other = lax.ppermute(mine, "dp", swap_core)
    kept = lax.all_to_all(attended, "tensor", split_axis=0, concat_axis=1, tiled=True)
    kept = kept.reshape(own_rows, ranks, 2, part)
    low = kept[:, :, 0].reshape(own_rows, ranks * part)
    high = kept[:, :, 1].reshape(own_rows, ranks * part)
    out = jnp.dot(
        jnp.where(core == 0, low, high), mine, preferred_element_type=jnp.float32
    ) + jnp.dot(jnp.where(core == 0, high, low), other, preferred_element_type=jnp.float32)
    return out.astype(jnp.bfloat16)[None]


PIECES = 2
SHARERS = 4
BLOCKS = 4
MESH = pl.DeviceIdType.MESH


def whole_layer(
    line, rows_ref, w_ref, ow_ref, fv_ref, table_ref, index_ref, length_ref, out_ref,
    hid, wts, wf_ref, kept, px_out, px_in, finished, qkv_ref, fo_ref, att, gathered_att,
    load_sem, w_sem, wy_sem, wd_sem, we_sem, a1_sem, a2_sem, a3_sem, cx_sem, cz_sem,
    oz_sem, ox_sem, oy_sem, od_sem, oe_sem, fv_sem, at_sem,
):
    group, core, rank = lax.axis_index("groups"), lax.axis_index("dp"), lax.axis_index("tensor")
    spot, side = rank // PAIR, rank % PAIR
    ranks = line * PAIR
    steps = line - 1
    own_rows, width = rows_ref.shape
    half = width // PAIR
    part = half // SHARERS
    head = w_ref.shape[2]
    piece = own_rows // PIECES
    quarter = head // SHARERS
    mine, across = group * 2 + core, (1 - group) * 2 + core
    sib_mine, sib_across = group * 2 + 1 - core, (1 - group) * 2 + 1 - core
    near = spot + 1 - 2 * (spot % 2)
    far = (spot + line // 2) % line
    left, right = (group, core, rank - PAIR), (group, core, rank + PAIR)
    partner = (group, core, spot * PAIR + 1 - side)
    rows_peer = (group, core, far * PAIR + side)
    heads_peer = (group, core, near * PAIR + side)
    opposite = (1 - group, core, rank)
    sibling = (group, 1 - core, rank)
    has_left, has_right = spot > 0, spot < steps

    barrier = pltpu.get_barrier_semaphore()
    peers = [(group, core, (rank + o) % ranks) for o in range(1, ranks)]
    for there in peers + [opposite, sibling]:
        pl.semaphore_signal(barrier, inc=1, device_id=there, device_id_type=MESH)

    def cut(index, size):
        return pl.ds(pl.multiple_of(index * size, size), size)

    def row_block(b, p=None):
        if p is None:
            return pl.ds(b * own_rows, own_rows)
        return pl.ds(b * own_rows + p * piece, piece)

    own_half, other_half = cut(side, half), cut(1 - side, half)
    loads = [
        pltpu.make_async_copy(rows_ref.at[:, own_half], hid.at[row_block(0), :], load_sem.at[0]),
        pltpu.make_async_copy(w_ref.at[:, own_half, :], wts.at[0, :, :, pl.ds(0, head)], load_sem.at[1]),
        pltpu.make_async_copy(ow_ref, wf_ref.at[cut(rank, head), :], load_sem.at[2]),
        pltpu.make_async_copy(fv_ref.at[:, cut(rank, head)], fo_ref.at[cut(rank, own_rows), :], load_sem.at[3]),
    ]
    for load in loads:
        load.start()
    pl.semaphore_wait(barrier, ranks + 1)

    def send(src, dst, sems, at, there):
        return pltpu.make_async_remote_copy(
            src_ref=src, dst_ref=dst, send_sem=sems.at[(0,) + at], recv_sem=sems.at[(1,) + at],
            device_id=there, device_id_type=MESH,
        )

    def wpart(kind, j, q):
        zone, lane = (0, 1) if kind == 0 else (1, kind - 1)
        return wts.at[zone, j, cut(q, part), pl.ds(lane * head, head)]

    def w_source(s, j):
        return w_ref.at[j, pl.ds(pl.multiple_of(s * half + mine * part, part), part), :]

    def w_first(kind, j):
        if kind == 0:
            return send(w_source(1 - side, j), wpart(0, j, mine), w_sem, (0, j), partner)
        source = w_source(side, j) if kind == 1 else wpart(0, j, mine)
        return send(source, wpart(kind, j, mine), w_sem, (kind, j), heads_peer)

    def w_across(kind, j, q):
        return send(wpart(kind, j, q), wpart(kind, j, q), wy_sem, (kind, j), opposite)

    def w_down(kind, j, q):
        return send(wpart(kind, j, q), wpart(kind, j, q), wd_sem, (kind, j), sibling)

    def w_echo(kind, j, q):
        return send(wpart(kind, j, q), wpart(kind, j, q), we_sem, (kind, j), sibling)

    def arr(kind, j):
        w_first(kind, j).wait_recv()
        if kind == 0:
            w_first(2, j).start()
        w_across(kind, j, mine).start()
        w_down(kind, j, mine).start()

    def pas(kind, j):
        w_across(kind, j, across).wait_recv()
        w_echo(kind, j, across).start()

    def w_ready(kind):
        for j in range(3):
            w_down(kind, j, sib_mine).wait_recv()
            w_echo(kind, j, sib_across).wait_recv()

    def a1(p):
        return send(
            rows_ref.at[pl.ds(p * piece, piece), other_half], hid.at[row_block(1, p), :], a1_sem, (p,), partner
        )

    def a2(p):
        return send(
            rows_ref.at[pl.ds(p * piece, piece), own_half], hid.at[row_block(2, p), :], a2_sem, (p,), rows_peer
        )

    def a3(p):
        return send(hid.at[row_block(1, p), :], hid.at[row_block(3, p), :], a3_sem, (p,), rows_peer)

    def fwd(p):
        a1(p).wait_recv()
        a3(p).start()

    def swapped(b):
        return b + 1 - 2 * (b % 2)

    def cx(e, b):
        return pltpu.make_async_remote_copy(
            src_ref=px_out.at[e, b], dst_ref=px_in.at[e, swapped(b)], send_sem=cx_sem.at[0, e, b],
            recv_sem=cx_sem.at[1, e, swapped(b)], device_id=partner, device_id_type=MESH,
        )

    def place(b):
        return cut((spot, far)[b // 2] * PAIR + (side, 1 - side)[b % 2], own_rows)

    def cz(b):
        return send(finished.at[b], qkv_ref.at[:, place(b), :], cz_sem, (b,), heads_peer)

    def project(e, first, count):
        def one(j, carry):
            total = jnp.dot(
                hid[pl.ds(first * own_rows, count * own_rows), :], wts[e, j],
                preferred_element_type=jnp.float32,
            )
            for i in range(count):
                rows = total[i * own_rows : (i + 1) * own_rows]
                kept[e, first + i, j] = rows[:, :head]
                px_out[e, first + i, j] = rows[:, head:].astype(jnp.bfloat16)
            return carry

        lax.fori_loop(0, 3, one, 0)
        for b in range(first, first + count):
            cx(e, b).start()

    def comb(e, b):
        cx(e, swapped(b)).wait_recv()
        total = (kept[e, b] + px_in[e, b].astype(jnp.float32)).astype(jnp.bfloat16)
        if e == 0:
            qkv_ref[:, place(b), :] = total
        else:
            finished[b] = total
            cz(b).start()

    def first_copy(o):
        return send(fv_ref.at[:, cut(peers[o][2], head)], fo_ref.at[cut(rank, own_rows), :], fv_sem, (o,), peers[o])

    def wf(column, q):
        return wf_ref.at[pl.ds(pl.multiple_of(column * head + q * quarter, quarter), quarter), :]

    def wf_half(column, c):
        return wf_ref.at[pl.ds(pl.multiple_of(column * head + c * (head // 2), head // 2), head // 2), :]

    def chunk(way, k):
        return spot - 1 - k if way == 0 else spot + 1 + k

    def arrives(way, k):
        return k < spot if way == 0 else spot + 1 + k < line

    def leaves(way, k):
        if way == 0:
            return jnp.logical_and(k <= spot, has_right)
        return jnp.logical_and(spot + k < line, has_left)

    def carried(way, k):
        return spot - k if way == 0 else spot + k

    def column_of(kind, way, k):
        at = chunk(way, k)
        return at * PAIR + (side if kind == 0 else 1 - side)

    def out_z(way, k, at):
        column = at * PAIR + side
        source = ow_ref.at[cut(mine, quarter), :] if k == 0 else wf(column, mine)
        return send(source, wf(column, mine), oz_sem, (way, k), right if way == 0 else left)

    def out_x(way, k, column):
        return send(wf(column, mine), wf(column, mine), ox_sem, (way, k), partner)

    def out_y(kind, way, k, q):
        column = column_of(kind, way, k)
        return send(wf(column, q), wf(column, q), oy_sem, (kind, way, k), opposite)

    def out_d(kind, way, k, q):
        column = column_of(kind, way, k)
        return send(wf(column, q), wf(column, q), od_sem, (kind, way, k), sibling)

    def out_e(kind, way, k, q):
        column = column_of(kind, way, k)
        return send(wf(column, q), wf(column, q), oe_sem, (kind, way, k), sibling)

    partner_column = spot * PAIR + 1 - side

    def out_partner():
        return send(ow_ref.at[cut(core, head // 2), :], wf_half(rank, core), ox_sem, (2, 0), partner)

    def out_shared(c):
        return send(wf_half(partner_column, c), wf_half(partner_column, c), ox_sem, (2, 1), sibling)

    def oxp():
        out_partner().wait_recv()
        out_shared(core).start()

    def out_begin():
        for way in (0, 1):

            @pl.when(leaves(way, 0))
            def _():
                out_z(way, 0, spot).start()

    def oz(way, k):
        @pl.when(arrives(way, k))
        def _():
            at = chunk(way, k)
            out_z(way, k, at).wait_recv()
            if k + 1 < steps:

                @pl.when(leaves(way, k + 1))
                def _():
                    out_z(way, k + 1, at).start()

            out_x(way, k, column_of(0, way, k)).start()
            out_y(0, way, k, mine).start()
            out_d(0, way, k, mine).start()

    def ox(way, k):
        @pl.when(arrives(way, k))
        def _():
            out_x(way, k, column_of(1, way, k)).wait_recv()
            out_y(1, way, k, mine).start()
            out_d(1, way, k, mine).start()

    def oe(kind, way, k):
        @pl.when(arrives(way, k))
        def _():
            out_y(kind, way, k, across).wait_recv()
            out_e(kind, way, k, across).start()

    def begin_fv():
        for o in range(ranks - 1):
            first_copy(o).start()

    def near_dots():
        for load in loads:
            load.wait()
        w_ready(0)
        project(0, 0, 2)

    def far_dots():
        w_ready(1)
        w_ready(2)
        project(1, 0, 2)

    def row_dots(b, copy):
        for p in range(PIECES):
            copy(p).wait_recv()
        project(1, b, 1)
        project(0, b, 1)

    total_rows = ranks * own_rows
    block_rows = PAIR * own_rows

    def att_copy(o, r, me):
        return send(
            att.at[cut(r, own_rows), :], gathered_att.at[:, cut(me, head)], at_sem, (o,), peers[o]
        )

    def attend():
        for b in range(BLOCKS):
            cz(b).wait_recv()
        for o in range(ranks - 1):
            first_copy(o).wait_recv()
        chosen_row = index_ref[0]
        now, before = table_ref[0, chosen_row], table_ref[1, chosen_row]
        valid = length_ref[0]
        values = (now * qkv_ref[2].astype(jnp.float32) + before * fo_ref[...].astype(jnp.float32)).astype(
            jnp.bfloat16
        )
        score_scale = 1.0 / math.sqrt(head)
        for first_row in range(0, total_rows, block_rows):
            stop = first_row + block_rows
            scores = lax.dot_general(
                qkv_ref[0, first_row:stop, :], qkv_ref[1, :stop, :], (((1,), (1,)), ((), ())),
                preferred_element_type=jnp.float32,
            ) * score_scale
            shape = (block_rows, stop)
            limit = jnp.minimum(lax.broadcasted_iota(jnp.int32, (block_rows, 1), 0) + (first_row + 1), valid)
            scores = jnp.where(lax.broadcasted_iota(jnp.int32, shape, 1) < limit, scores, NEG_FILL)
            raised = jnp.exp(scores - jnp.max(scores, axis=1, keepdims=True))
            weights = (raised / jnp.sum(raised, axis=1, keepdims=True)).astype(jnp.bfloat16)
            att[first_row:stop, :] = jnp.dot(
                weights, values[:stop], preferred_element_type=jnp.float32
            ).astype(jnp.bfloat16)
        for o in range(ranks - 1):
            att_copy(o, peers[o][2], rank).start()
        own = pltpu.make_async_copy(
            att.at[cut(rank, own_rows), :], gathered_att.at[:, cut(rank, head)], load_sem.at[0]
        )
        own.start()
        own.wait()

    def each_column(action):
        for k in range(steps):
            for way in (0, 1):

                @pl.when(arrives(way, k))
                def _():
                    for kind in (0, 1):
                        action(kind, way, k)

    def column_in(kind, way, k):
        out_d(kind, way, k, sib_mine).wait_recv()
        out_e(kind, way, k, sib_across).wait_recv()

    def finish():
        for o in range(ranks - 1):
            att_copy(o, 0, (rank + ranks - 1 - o) % ranks).wait_recv()
        each_column(column_in)
        out_shared(1 - core).wait_recv()
        wide = width // (2 * PIECES * PAIR) if width % (1024 * PIECES) == 0 else width

        def one(i, carry):
            at = pl.ds(pl.multiple_of(i * wide, wide), wide)
            out_ref[:, at] = jnp.dot(
                gathered_att[...], wf_ref[:, at], preferred_element_type=jnp.float32
            ).astype(jnp.bfloat16)
            return carry

        lax.fori_loop(0, width // wide, one, 0)

    def drain():
        for p in range(PIECES):
            a1(p).wait_send()
            a2(p).wait_send()
            a3(p).wait_send()
        for kind in range(3):
            for j in range(3):
                w_first(kind, j).wait_send()
                w_across(kind, j, mine).wait_send()
                w_down(kind, j, mine).wait_send()
                w_echo(kind, j, across).wait_send()
        for e in range(2):
            for b in range(BLOCKS):
                cx(e, b).wait_send()
        for b in range(BLOCKS):
            cz(b).wait_send()
        for o in range(ranks - 1):
            first_copy(o).wait_send()
            att_copy(o, peers[o][2], rank).wait_send()
        out_partner().wait_send()
        out_shared(core).wait_send()

        def column_out(kind, way, k):
            if kind == 0:
                out_x(way, k, column_of(0, way, k)).wait_send()
            out_y(kind, way, k, mine).wait_send()
            out_d(kind, way, k, mine).wait_send()
            out_e(kind, way, k, across).wait_send()

        each_column(column_out)
        for k in range(steps):
            for way in (0, 1):

                @pl.when(leaves(way, k))
                def _():
                    out_z(way, k, carried(way, k)).wait_send()

    out_begin()
    w_first(0, 0).start()

    @pl.when(core == 0)
    def _():
        w_first(0, 1).start()
        w_first(0, 2).start()
        a1(0).start()
        a1(1).start()
        a2(0).start()
        w_first(1, 0).start()
        w_first(1, 1).start()
        a2(1).start()
        w_first(1, 2).start()

    @pl.when(core == 1)
    def _():
        a1(0).start()
        w_first(0, 1).start()
        a1(1).start()
        w_first(0, 2).start()
        w_first(1, 0).start()
        w_first(1, 1).start()
        w_first(1, 2).start()
        a2(0).start()
        a2(1).start()

    arr(0, 0)
    arr(0, 1)
    oz(1, 0)
    pas(0, 0)
    arr(1, 0)
    oz(0, 0)
    fwd(0)
    oe(0, 0, 0)
    arr(0, 2)
    pas(0, 1)
    oe(0, 1, 0)
    arr(1, 1)
    pas(1, 0)
    fwd(1)
    out_partner().start()
    begin_fv()
    pas(0, 2)
    arr(1, 2)
    near_dots()
    ox(0, 0)
    ox(1, 0)
    oe(1, 0, 0)
    arr(2, 0)
    oz(1, 1)
    pas(1, 2)
    oz(0, 1)
    arr(2, 1)
    oxp()
    pas(1, 1)
    oe(1, 1, 0)
    pas(2, 0)
    comb(0, 1)
    comb(0, 0)
    oe(0, 1, 1)
    oe(0, 0, 1)
    arr(2, 2)
    pas(2, 1)
    ox(1, 1)
    ox(0, 1)
    pas(2, 2)
    far_dots()
    row_dots(2, a2)
    oe(1, 0, 1)
    oz(0, 2)
    oe(1, 1, 1)
    oz(1, 2)
    comb(1, 1)
    comb(1, 0)
    row_dots(3, a3)
    comb(1, 3)
    comb(0, 3)
    oe(0, 1, 2)
    oe(0, 0, 2)
    ox(1, 2)
    comb(1, 2)
    comb(0, 2)
    ox(0, 2)
    attend()
    oe(1, 0, 2)
    oe(1, 1, 2)
    finish()
    drain()


def fused(local_rows, w3, out_weight, firsts, mix_table, mix_index, lengths, ranks):
    line = ranks // PAIR
    steps = line - 1
    own_rows, width = local_rows.shape
    head_width = w3.shape[2]
    half = width // PAIR
    kind = local_rows.dtype
    total_rows = ranks * own_rows
    dma = pltpu.SemaphoreType.DMA
    anywhere = pl.BlockSpec(memory_space=pltpu.HBM)
    scalars = pl.BlockSpec(memory_space=pltpu.SMEM)
    tile = (2, BLOCKS, 3, own_rows, head_width)
    return pl.pallas_call(
        functools.partial(whole_layer, line),
        out_shape=jax.ShapeDtypeStruct((own_rows, width), kind),
        in_specs=[anywhere] * 4 + [scalars] * 3,
        out_specs=pl.BlockSpec(memory_space=pltpu.VMEM),
        scratch_shapes=[
            pltpu.VMEM((BLOCKS * own_rows, half), kind),
            pltpu.VMEM((2, 3, half, 2 * head_width), kind),
            pltpu.VMEM((ranks * head_width, width), kind),
            pltpu.VMEM(tile, jnp.float32),
            pltpu.VMEM(tile, kind),
            pltpu.VMEM(tile, kind),
            pltpu.VMEM(tile[1:], kind),
            pltpu.VMEM((3, total_rows, head_width), kind),
            pltpu.VMEM((total_rows, head_width), kind),
            pltpu.VMEM((total_rows, head_width), kind),
            pltpu.VMEM((own_rows, ranks * head_width), kind),
            dma((4,)),
            dma((2, 3, 3)), dma((2, 3, 3)), dma((2, 3, 3)), dma((2, 3, 3)),
            dma((2, PIECES)), dma((2, PIECES)), dma((2, PIECES)),
            dma((2, 2, BLOCKS)), dma((2, BLOCKS)),
            dma((2, 2, steps)), dma((2, 3, steps)),
            dma((2, 2, 2, steps)), dma((2, 2, 2, steps)), dma((2, 2, 2, steps)),
            dma((2, ranks - 1)), dma((2, ranks - 1)),
        ],
        compiler_params=pltpu.CompilerParams(
            collective_id=0, has_side_effects=True, vmem_limit_bytes=60 * 1024 * 1024
        ),
    )(local_rows, w3, out_weight, firsts, mix_table, mix_index, lengths)


def body_fused(hidden_in, first_values, qkv_weight, out_weight, mix_table, mix_index, lengths):
    return fused(
        hidden_in[0], qkv_weight.transpose(1, 0, 2), out_weight, first_values[0],
        mix_table.T, mix_index, lengths, lax.axis_size("tensor"),
    )[None]


def chosen(hidden_in, first_values, qkv_weight, out_weight, mix_table, mix_index, lengths):
    args = (hidden_in, first_values, qkv_weight, out_weight, mix_table, mix_index, lengths)
    ranks = lax.axis_size("tensor")
    total_rows = ranks * hidden_in.shape[1]
    fits = ranks * out_weight.size * 2 <= total_rows * hidden_in.shape[2] * 4
    two = lax.axis_size("groups") == 2 and lax.axis_size("dp") == 2
    pairs = ranks == BLOCKS * PAIR and hidden_in.shape[2] % (SHARERS * PAIR * 128) == 0
    single = mix_index.shape[0] == 1 and qkv_weight.shape[2] == 128
    if fits and two and pairs and single:
        return body_fused(*args)
    return body(*args)


def solution(mesh):
    placed = (
        P(("groups", "dp"), "tensor", None),
        P(("groups", "dp"), "tensor", None),
        P(None, None, "tensor"),
        P("tensor", None),
        P(),
        P("tensor"),
        P(("groups", "dp")),
    )
    return jax.shard_map(
        chosen,
        mesh=mesh,
        in_specs=placed,
        out_specs=P(("groups", "dp"), "tensor", None),
        check_vma=False,
    )
```

time: 146 us -> 118 us (0.81)
  Pallas kernels: 133 us -> 114 us
  matrix products: 4.82 us -> 0 us
  other arithmetic: 2.17 us -> 0 us
  local copies, waits for them, and re-layouts: 4.27 us -> 2.46 us
    pallas_call x2 -> x1, Pallas kernels: 133 us -> 114 us  [fused(): pl.pallas_call(functools.partial(whole_layer, line), out_shape=jax.ShapeD...]
    dot_general x6 -> x0, matrix products: 4.82 us -> none  [the longest x1 2.59 us: body_gathered(): jnp.dot(kept, weights, preferred_element_type=jnp.float32)]
    unnamed x16 -> x1, local copies, waits for them, and re-layouts: 3.6 us -> 2.46 us
where the time goes in v1:
time: 118 us
  Pallas kernels  114 us (97%)
  local copies, waits for them, and re-layouts  2.46 us (2%)
  between operations  1.3 us (1%)
    pallas_call x1, Pallas kernels, fused(): pl.pallas_call(functools.partial(whole_layer, line), out_shape=jax.ShapeD...  114 us
    unnamed x1, local copies, waits for them, and re-layouts  2.46 us

profile of v1, /device:TPU:0, one launch (start us, length us, event | category | flops | bytes accessed | tf_op | source)
XLA Modules:
  0.0 117.6 jit_solution(5156070948588177321)
XLA Ops:
  1.3 113.8 %shard_map.73 = bf16[128,5120]{1,0:T(8,128)(2,1)} custom-call(bf16[128,5120]{1,0:T(8,128)(2,1)} %bitcast.7, bf16[3,5120,128]{2,1,0:T(8,128)(2,1)} %bitcast.6, bf16[128,5120]{1,0:T(8,128)(2,1)} %ow_ref.1, bf16[128,1024]{1,0:T(8,128)(2,1)} %bitcast.8, f32[2,8]{1,0:T(2,128)} %bitcast.9, s32[1]{0:T(128)S(6)} %copy.9.index_ref, s32[1]{0:T(128)S(6)} %copy.10.length_ref), custom_call_target="tpu_custom_call" | custom-call | tf_op jit(solution)/shard_map/pallas_call | solution.py:612
  115.2 2.5 %copy.11 = bf16[1,128,5120]{2,1,0:T(8,128)(2,1)} copy(bf16[1,128,5120]{2,1,0:T(8,128)(2,1)} %bitcast.5) | data formatting | bytes 2621440

commit v2 on v1

--- a/solution.py
+++ b/solution.py
@@ -132,7 +132,7 @@
 
 def whole_layer(
     line, rows_ref, w_ref, ow_ref, fv_ref, table_ref, index_ref, length_ref, out_ref,
-    hid, wts, wf_ref, kept, px_out, px_in, finished, qkv_ref, fo_ref, att, gathered_att,
+    hid, wts, wf_ref, kept, px_out, px_in, finished, qkv_ref, fo_ref, att, gathered_att, levels,
     load_sem, w_sem, wy_sem, wd_sem, we_sem, a1_sem, a2_sem, a3_sem, cx_sem, cz_sem,
     oz_sem, ox_sem, oy_sem, od_sem, oe_sem, fv_sem, at_sem,
 ):
@@ -177,6 +177,7 @@
         pltpu.make_async_copy(w_ref.at[:, own_half, :], wts.at[0, :, :, pl.ds(0, head)], load_sem.at[1]),
         pltpu.make_async_copy(ow_ref, wf_ref.at[cut(rank, head), :], load_sem.at[2]),
         pltpu.make_async_copy(fv_ref.at[:, cut(rank, head)], fo_ref.at[cut(rank, own_rows), :], load_sem.at[3]),
+        pltpu.make_async_copy(table_ref, levels, load_sem.at[4]),
     ]
     for load in loads:
         load.start()
@@ -387,24 +388,49 @@
         w_ready(0)
         project(0, 0, 2)
 
+    def row_dots():
+        for p in range(PIECES):
+            a2(p).wait_recv()
+        project(0, 2, 1)
+
     def far_dots():
         w_ready(1)
         w_ready(2)
-        project(1, 0, 2)
-
-    def row_dots(b, copy):
+        project(1, 0, 3)
+
+    def last_dots():
         for p in range(PIECES):
-            copy(p).wait_recv()
-        project(1, b, 1)
-        project(0, b, 1)
+            a3(p).wait_recv()
+        project(1, 3, 1)
+        project(0, 3, 1)
 
     total_rows = ranks * own_rows
     block_rows = PAIR * own_rows
 
-    def att_copy(o, r, me):
-        return send(
-            att.at[cut(r, own_rows), :], gathered_att.at[:, cut(me, head)], at_sem, (o,), peers[o]
-        )
+    def att_copy(r):
+        return pltpu.make_async_remote_copy(
+            src_ref=att.at[pl.ds(r * own_rows, own_rows), :], dst_ref=gathered_att.at[:, cut(rank, head)],
+            send_sem=at_sem.at[0, r], recv_sem=at_sem.at[1, rank], device_id=(group, core, r), device_id_type=MESH,
+        )
+
+    def att_arrival(r):
+        return pltpu.make_async_remote_copy(
+            src_ref=att.at[pl.ds(r * own_rows, own_rows), :],
+            dst_ref=gathered_att.at[:, pl.ds(r * head, head)],
+            send_sem=at_sem.at[0, r], recv_sem=at_sem.at[1, r], device_id=(group, core, r), device_id_type=MESH,
+        )
+
+    def att_own():
+        return pltpu.make_async_copy(
+            att.at[cut(rank, own_rows), :], gathered_att.at[:, cut(rank, head)], load_sem.at[0]
+        )
+
+    def others(action):
+        for r in range(ranks):
+
+            @pl.when(rank != r)
+            def _():
+                action(r)
 
     def attend():
         for b in range(BLOCKS):
@@ -412,7 +438,7 @@
         for o in range(ranks - 1):
             first_copy(o).wait_recv()
         chosen_row = index_ref[0]
-        now, before = table_ref[0, chosen_row], table_ref[1, chosen_row]
+        now, before = levels[0, chosen_row], levels[1, chosen_row]
         valid = length_ref[0]
         values = (now * qkv_ref[2].astype(jnp.float32) + before * fo_ref[...].astype(jnp.float32)).astype(
             jnp.bfloat16
@@ -432,13 +458,13 @@
             att[first_row:stop, :] = jnp.dot(
                 weights, values[:stop], preferred_element_type=jnp.float32
             ).astype(jnp.bfloat16)
-        for o in range(ranks - 1):
-            att_copy(o, peers[o][2], rank).start()
-        own = pltpu.make_async_copy(
-            att.at[cut(rank, own_rows), :], gathered_att.at[:, cut(rank, head)], load_sem.at[0]
-        )
-        own.start()
-        own.wait()
+            for r in range(first_row // own_rows, stop // own_rows):
+
+                @pl.when(rank != r)
+                def _():
+                    att_copy(r).start()
+
+        att_own().start()
 
     def each_column(action):
         for k in range(steps):
@@ -454,8 +480,8 @@
         out_e(kind, way, k, sib_across).wait_recv()
 
     def finish():
-        for o in range(ranks - 1):
-            att_copy(o, 0, (rank + ranks - 1 - o) % ranks).wait_recv()
+        att_own().wait()
+        others(lambda r: att_arrival(r).wait_recv())
         each_column(column_in)
         out_shared(1 - core).wait_recv()
         wide = width // (2 * PIECES * PAIR) if width % (1024 * PIECES) == 0 else width
@@ -487,7 +513,7 @@
             cz(b).wait_send()
         for o in range(ranks - 1):
             first_copy(o).wait_send()
-            att_copy(o, peers[o][2], rank).wait_send()
+        others(lambda r: att_copy(r).wait_send())
         out_partner().wait_send()
         out_shared(core).wait_send()
 
@@ -506,93 +532,327 @@
                 def _():
                     out_z(way, k, carried(way, k)).wait_send()
 
-    out_begin()
-    w_first(0, 0).start()
-
-    @pl.when(core == 0)
-    def _():
+    ends = jnp.logical_or(spot == 0, spot == steps)
+    places = [
+        jnp.logical_and(ends, core == 0), jnp.logical_and(ends, core == 1),
+        jnp.logical_and(jnp.logical_not(ends), core == 0), jnp.logical_and(jnp.logical_not(ends), core == 1),
+    ]
+
+    @pl.when(places[0])
+    def _():
+        w_first(0, 0).start()
         w_first(0, 1).start()
         w_first(0, 2).start()
         a1(0).start()
         a1(1).start()
-        a2(0).start()
-        w_first(1, 0).start()
-        w_first(1, 1).start()
-        a2(1).start()
-        w_first(1, 2).start()
-
-    @pl.when(core == 1)
-    def _():
-        a1(0).start()
-        w_first(0, 1).start()
-        a1(1).start()
-        w_first(0, 2).start()
+        out_begin()
         w_first(1, 0).start()
         w_first(1, 1).start()
         w_first(1, 2).start()
         a2(0).start()
         a2(1).start()
-
-    arr(0, 0)
-    arr(0, 1)
-    oz(1, 0)
-    pas(0, 0)
-    arr(1, 0)
-    oz(0, 0)
-    fwd(0)
-    oe(0, 0, 0)
-    arr(0, 2)
-    pas(0, 1)
-    oe(0, 1, 0)
-    arr(1, 1)
-    pas(1, 0)
-    fwd(1)
-    out_partner().start()
-    begin_fv()
-    pas(0, 2)
-    arr(1, 2)
+        arr(0, 0)
+        arr(0, 1)
+        oz(0, 0)
+        oz(1, 0)
+        arr(0, 2)
+        out_partner().start()
+        pas(0, 1)
+        arr(1, 0)
+        fwd(0)
+        pas(0, 0)
+        oe(0, 0, 0)
+        arr(1, 1)
+        oe(0, 1, 0)
+        fwd(1)
+        pas(0, 2)
+        arr(1, 2)
+        pas(1, 1)
+        pas(1, 0)
+        ox(1, 0)
+
+    @pl.when(places[1])
+    def _():
+        a1(0).start()
+        w_first(0, 0).start()
+        a1(1).start()
+        w_first(0, 1).start()
+        w_first(0, 2).start()
+        out_begin()
+        a2(0).start()
+        w_first(1, 0).start()
+        w_first(1, 1).start()
+        w_first(1, 2).start()
+        a2(1).start()
+        arr(0, 0)
+        oz(0, 0)
+        pas(0, 0)
+        oz(1, 0)
+        fwd(0)
+        oe(0, 0, 0)
+        arr(1, 0)
+        arr(0, 1)
+        oe(0, 1, 0)
+        arr(0, 2)
+        out_partner().start()
+        pas(1, 0)
+        arr(1, 1)
+        pas(0, 1)
+        fwd(1)
+        pas(0, 2)
+
+    @pl.when(places[2])
+    def _():
+        w_first(0, 0).start()
+        w_first(0, 1).start()
+        a1(0).start()
+        a1(1).start()
+        w_first(0, 2).start()
+        out_begin()
+        w_first(1, 0).start()
+        w_first(1, 1).start()
+        w_first(1, 2).start()
+        a2(0).start()
+        a2(1).start()
+        arr(0, 0)
+        oz(1, 0)
+        oz(0, 0)
+        arr(0, 1)
+        pas(0, 0)
+        arr(1, 0)
+        fwd(0)
+        arr(1, 1)
+        fwd(1)
+        oe(0, 0, 0)
+        pas(0, 1)
+        arr(0, 2)
+        out_partner().start()
+        oe(0, 1, 0)
+        pas(1, 1)
+        pas(1, 0)
+        ox(0, 0)
+        pas(0, 2)
+        ox(1, 0)
+        arr(1, 2)
+
+    @pl.when(places[3])
+    def _():
+        w_first(0, 0).start()
+        a1(0).start()
+        w_first(0, 1).start()
+        a1(1).start()
+        w_first(0, 2).start()
+        out_begin()
+        w_first(1, 0).start()
+        w_first(1, 1).start()
+        a2(0).start()
+        a2(1).start()
+        w_first(1, 2).start()
+        arr(0, 0)
+        oz(1, 0)
+        arr(0, 1)
+        arr(1, 1)
+        oz(0, 0)
+        pas(0, 0)
+        fwd(0)
+        arr(1, 0)
+        arr(1, 2)
+        arr(0, 2)
+        out_partner().start()
+        pas(0, 1)
+        oe(0, 1, 0)
+        fwd(1)
+        oe(0, 0, 0)
+        pas(1, 0)
+        pas(1, 1)
+        ox(1, 0)
+        pas(1, 2)
+        pas(0, 2)
+        ox(0, 0)
+
     near_dots()
-    ox(0, 0)
-    ox(1, 0)
-    oe(1, 0, 0)
-    arr(2, 0)
-    oz(1, 1)
-    pas(1, 2)
-    oz(0, 1)
-    arr(2, 1)
-    oxp()
-    pas(1, 1)
-    oe(1, 1, 0)
-    pas(2, 0)
-    comb(0, 1)
-    comb(0, 0)
-    oe(0, 1, 1)
-    oe(0, 0, 1)
-    arr(2, 2)
-    pas(2, 1)
-    ox(1, 1)
-    ox(0, 1)
-    pas(2, 2)
+
+    @pl.when(places[0])
+    def _():
+        pas(1, 2)
+        arr(2, 0)
+
+    @pl.when(places[1])
+    def _():
+        pas(1, 1)
+        arr(1, 2)
+        ox(0, 0)
+        ox(1, 0)
+        arr(2, 0)
+        pas(1, 2)
+
+    row_dots()
+
+    @pl.when(places[0])
+    def _():
+        oe(1, 1, 0)
+        ox(0, 0)
+        oe(1, 0, 0)
+        pas(2, 0)
+        oz(1, 1)
+        arr(2, 1)
+        oz(0, 1)
+        oxp()
+        pas(2, 1)
+        comb(0, 1)
+        oe(0, 1, 1)
+        comb(0, 0)
+        oe(0, 0, 1)
+        arr(2, 2)
+        begin_fv()
+        pas(2, 2)
+
+    @pl.when(places[1])
+    def _():
+        oe(1, 0, 0)
+        oe(1, 1, 0)
+        pas(2, 0)
+        arr(2, 1)
+        oz(1, 1)
+        oxp()
+        oz(0, 1)
+        pas(2, 1)
+        oe(0, 1, 1)
+        comb(0, 0)
+        oe(0, 0, 1)
+        arr(2, 2)
+        begin_fv()
+        pas(2, 2)
+        oz(0, 2)
+        ox(0, 1)
+
+    @pl.when(places[2])
+    def _():
+        oz(1, 1)
+        arr(2, 1)
+        arr(2, 0)
+        arr(2, 2)
+        begin_fv()
+        oz(0, 1)
+        oe(1, 1, 0)
+        pas(1, 2)
+        oxp()
+        pas(2, 1)
+        pas(2, 0)
+        oe(1, 0, 0)
+        comb(0, 1)
+        comb(0, 0)
+        pas(2, 2)
+        ox(1, 1)
+        oe(0, 1, 1)
+        ox(0, 1)
+        oe(0, 0, 1)
+
+    @pl.when(places[3])
+    def _():
+        oz(1, 1)
+        arr(2, 0)
+        oe(1, 1, 0)
+        oz(0, 1)
+        oe(1, 0, 0)
+        oxp()
+        comb(0, 1)
+        pas(2, 0)
+        comb(0, 0)
+        arr(2, 1)
+        oe(0, 0, 1)
+        arr(2, 2)
+        begin_fv()
+        pas(2, 1)
+        oe(0, 1, 1)
+        ox(0, 1)
+        pas(2, 2)
+
     far_dots()
-    row_dots(2, a2)
-    oe(1, 0, 1)
-    oz(0, 2)
-    oe(1, 1, 1)
-    oz(1, 2)
-    comb(1, 1)
-    comb(1, 0)
-    row_dots(3, a3)
-    comb(1, 3)
-    comb(0, 3)
-    oe(0, 1, 2)
-    oe(0, 0, 2)
-    ox(1, 2)
-    comb(1, 2)
-    comb(0, 2)
-    ox(0, 2)
+
+    @pl.when(places[0])
+    def _():
+        ox(0, 1)
+        ox(1, 1)
+        comb(1, 1)
+        comb(1, 0)
+        oz(0, 2)
+        oe(1, 1, 1)
+        oz(1, 2)
+        oe(1, 0, 1)
+
+    @pl.when(places[1])
+    def _():
+        ox(1, 1)
+        comb(1, 1)
+        comb(1, 0)
+        oe(1, 0, 1)
+        oe(1, 1, 1)
+        comb(0, 1)
+        oz(1, 2)
+
+    @pl.when(places[3])
+    def _():
+        ox(1, 1)
+        comb(1, 1)
+
+    last_dots()
+
+    @pl.when(places[0])
+    def _():
+        comb(1, 3)
+        comb(0, 3)
+        oe(0, 1, 2)
+        ox(0, 2)
+        comb(1, 2)
+        oe(0, 0, 2)
+        ox(1, 2)
+        comb(0, 2)
+        oe(1, 0, 2)
+
+    @pl.when(places[1])
+    def _():
+        oe(0, 0, 2)
+        ox(0, 2)
+        comb(0, 3)
+        comb(1, 3)
+        oe(0, 1, 2)
+        ox(1, 2)
+        comb(1, 2)
+        comb(0, 2)
+        oe(1, 1, 2)
+
+    @pl.when(places[2])
+    def _():
+        oe(1, 0, 1)
+        comb(1, 1)
+        oe(1, 1, 1)
+        comb(1, 0)
+        comb(1, 3)
+        comb(0, 3)
+        comb(1, 2)
+        comb(0, 2)
+
+    @pl.when(places[3])
+    def _():
+        comb(0, 3)
+        comb(1, 0)
+        oe(1, 0, 1)
+        comb(1, 3)
+        oe(1, 1, 1)
+        comb(1, 2)
+        comb(0, 2)
+
     attend()
-    oe(1, 0, 2)
-    oe(1, 1, 2)
+
+    @pl.when(places[0])
+    def _():
+        oe(1, 1, 2)
+
+    @pl.when(places[1])
+    def _():
+        oe(1, 0, 2)
+
     finish()
     drain()
 
@@ -609,10 +869,11 @@
     anywhere = pl.BlockSpec(memory_space=pltpu.HBM)
     scalars = pl.BlockSpec(memory_space=pltpu.SMEM)
     tile = (2, BLOCKS, 3, own_rows, head_width)
+    held = (local_rows, w3, out_weight, firsts, mix_table)
     return pl.pallas_call(
         functools.partial(whole_layer, line),
         out_shape=jax.ShapeDtypeStruct((own_rows, width), kind),
-        in_specs=[anywhere] * 4 + [scalars] * 3,
+        in_specs=[anywhere] * 5 + [scalars] * 2,
         out_specs=pl.BlockSpec(memory_space=pltpu.VMEM),
         scratch_shapes=[
             pltpu.VMEM((BLOCKS * own_rows, half), kind),
@@ -626,18 +887,19 @@
             pltpu.VMEM((total_rows, head_width), kind),
             pltpu.VMEM((total_rows, head_width), kind),
             pltpu.VMEM((own_rows, ranks * head_width), kind),
-            dma((4,)),
+            pltpu.SMEM(mix_table.shape, mix_table.dtype),
+            dma((5,)),
             dma((2, 3, 3)), dma((2, 3, 3)), dma((2, 3, 3)), dma((2, 3, 3)),
             dma((2, PIECES)), dma((2, PIECES)), dma((2, PIECES)),
             dma((2, 2, BLOCKS)), dma((2, BLOCKS)),
             dma((2, 2, steps)), dma((2, 3, steps)),
             dma((2, 2, 2, steps)), dma((2, 2, 2, steps)), dma((2, 2, 2, steps)),
-            dma((2, ranks - 1)), dma((2, ranks - 1)),
+            dma((2, ranks - 1)), dma((2, ranks)),
         ],
         compiler_params=pltpu.CompilerParams(
-            collective_id=0, has_side_effects=True, vmem_limit_bytes=60 * 1024 * 1024
+            collective_id=0, has_side_effects=True, vmem_limit_bytes=52 * 1024 * 1024
         ),
-    )(local_rows, w3, out_weight, firsts, mix_table, mix_index, lengths)
+    )(*[pltpu.with_memory_space_constraint(a, pltpu.HBM) for a in held], mix_index, lengths)
 
 
 def body_fused(hidden_in, first_values, qkv_weight, out_weight, mix_table, mix_index, lengths):

time: 118 us -> 111 us (0.941)
  Pallas kernels: 114 us -> 109 us
  local copies, waits for them, and re-layouts: 2.46 us -> 1.06 us
    pallas_call x1, Pallas kernels: 114 us -> 109 us  [fused(): pl.pallas_call(functools.partial(whole_layer, line), out_shape=jax.ShapeD...]
    unnamed x1, local copies, waits for them, and re-layouts: 2.46 us -> 1.06 us
where the time goes in v2:
time: 111 us
  Pallas kernels  109 us (98%)
  between operations  1.3 us (1%)
    pallas_call x1, Pallas kernels, fused(): pl.pallas_call(functools.partial(whole_layer, line), out_shape=jax.ShapeD...  109 us

profile of v2, /device:TPU:0, one launch (start us, length us, event | category | flops | bytes accessed | tf_op | source)
XLA Modules:
  0.0 111.2 jit_solution(11981528043736523600)
XLA Ops:
  1.3 108.8 %shard_map.73 = bf16[128,5120]{1,0:T(8,128)(2,1)S(1)} custom-call(bf16[128,5120]{1,0:T(8,128)(2,1)} %bitcast.7, bf16[3,5120,128]{2,1,0:T(8,128)(2,1)} %bitcast.6, bf16[128,5120]{1,0:T(8,128)(2,1)} %ow_ref.1, bf16[128,1024]{1,0:T(8,128)(2,1)} %bitcast.8, f32[2,8]{1,0:T(2,128)} %bitcast.9, s32[1]{0:T(128)S(6)} %copy.9.index_ref, s32[1]{0:T(128)S(6)} %copy.10.length_ref), custom_call_target="tpu_custom_call" | custom-call | tf_op jit(solution)/shard_map/pallas_call | solution.py:873
  110.1 1.1 copy.11
